TPU v7x, 32 devices: a whole 2x2x4 slice. The times are simulated.
32 devices in a mesh: grp: 2 (over x), wide: 16 (over z, y, core).
Axes of the slice: x: 2, y: 2, z: 4, core: 2. Of those that a mesh axis runs over, the one named last changes fastest.
Arguments:
- kv_prefill: bfloat16 [2, 16, 8, 8192, 128], P(None, 'grp', None, 'wide'), parts along dimension 1, may hold values from -4 to 4
- queries: bfloat16 [128, 1024], P(('grp', 'wide')), parts along dimension 0, may hold values from -512 to 512
- fresh_kv: bfloat16 [2, 128, 128], P(None, ('grp', 'wide')), parts along dimension 1, may hold values from -4 to 4
- lengths: int32 [16], P('grp'), parts along dimension 0, may hold values from 1 to 8191, as said below
- decode_slot_pair: int32 [128], P('grp'), parts along dimension 0, may hold values from 0 to 63, each once
Outputs:
- decode_cache: bfloat16 [2, 128, 8192, 128], P(None, ('grp', 'wide')), parts along dimension 1
- attention: bfloat16 [128, 1024], P(('grp', 'wide')), parts along dimension 0
There are 2 independent parts, one for each index of `grp`. A program takes and returns all parts, laid end to end along the dimension named above; each array names one. Nothing has to cross between parts.
Inputs may be any that keep to these rules, and one draw needn't show every extreme that they name: `lengths`: every draw holds a sequence of length 8191 and one of length 1. `decode_slot_pair`: slot j lies on the device of wide with index j // (64 / 16).
All inputs are finite; a program needn't handle non-finite values.
Results may differ from a plain program's by a relative error of at most 0.001.
Values may be sent and summed in bfloat16 or wider, within the bound.
No kernel may reach another device: no remote copies, remote signals or barrier semaphores. Data moves between devices by JAX's collectives and lax.ppermute only.
A program may use at most 128 MiB of HBM per device.

v0:
```python
import functools
import math

import jax
import jax.numpy as jnp
from jax import lax
from jax.experimental import pallas as pl
from jax.experimental.pallas import tpu as pltpu
from jax.sharding import PartitionSpec as P

NEG_FILL = -1e30


def rank_of(limits, rows_start):
    held, ranks, count = [], [], 0
    for limit in limits:
        some = (limit > rows_start).astype(jnp.int32)
        held.append(some)
        ranks.append(count)
        count = count + some
    return held, ranks


def slot_lengths(slots_ref, lengths_ref, device, per_device, head_count):
    items = [slots_ref[device * per_device + slot] for slot in range(per_device)]
    return items, [lengths_ref[item // head_count] for item in items]


def gather_body(
    offset, per_device, head_count, dense, me_ref, slots_ref, lengths_ref, kv_ref, sent_ref, held_ref, in_sem, out_sem
):
    rows = kv_ref.shape[2]
    me = me_ref[0]
    items, limits = slot_lengths(slots_ref, lengths_ref, me ^ offset, per_device, head_count)
    held, ranks = rank_of(limits, me * rows)
    total = ranks[-1] + held[-1]
    for unit in range(per_device):
        if dense:
            item = items[unit]
        else:
            item = items[0]
            for slot in range(per_device):
                place = jnp.where(held[slot] == 1, ranks[slot], total + slot - ranks[slot])
                item = jnp.where(place == unit, items[slot], item)
        pltpu.make_async_copy(kv_ref.at[:, item], held_ref.at[unit], in_sem.at[unit]).start()
    for unit in range(per_device):
        pltpu.make_async_copy(kv_ref.at[:, 0], held_ref.at[unit], in_sem.at[unit]).wait()
        pltpu.make_async_copy(held_ref.at[unit], sent_ref.at[unit], out_sem.at[unit]).start()
    for unit in range(per_device):
        pltpu.make_async_copy(held_ref.at[unit], sent_ref.at[unit], out_sem.at[unit]).wait()


def gather_units(scalars, kv, offset, per_device, head_count, dense):
    _, _, rows, head_dim = kv.shape
    unit = (2, rows, head_dim)
    return pl.pallas_call(
        functools.partial(gather_body, offset, per_device, head_count, dense),
        out_shape=jax.ShapeDtypeStruct((per_device, *unit), kv.dtype),
        grid_spec=pltpu.PrefetchScalarGridSpec(
            num_scalar_prefetch=3,
            grid=(1,),
            in_specs=[pl.BlockSpec(memory_space=pl.ANY)],
            out_specs=pl.BlockSpec(memory_space=pl.ANY),
            scratch_shapes=[
                pltpu.VMEM((per_device, *unit), kv.dtype),
                pltpu.SemaphoreType.DMA((per_device,)),
                pltpu.SemaphoreType.DMA((per_device,)),
            ],
        ),
        cost_estimate=pl.CostEstimate(
            flops=per_device * 2 * rows * head_dim * 16,
            bytes_accessed=4 * per_device * 2 * rows * head_dim,
            transcendentals=0,
        ),
        name="gather_units",
    )(*scalars, kv)


def absorb_body(
    offset, per_device, head_count, scale, dense, first, last, me_ref, slots_ref, lengths_ref, recv_ref, *refs
):
    if first:
        token_ref, cache_ref, state_ref, held_ref, in_sem, out_sem = refs
    else:
        token_ref, _, old_ref, cache_ref, state_ref, held_ref, in_sem, out_sem = refs
    me = me_ref[0]
    rows, head_dim = held_ref.shape[-2:]
    group = token_ref.shape[1] - 2
    start = (me ^ offset) * rows
    _, limits = slot_lengths(slots_ref, lengths_ref, me, per_device, head_count)
    held, ranks = rank_of(limits, start)
    for slot in range(per_device):
        unit = slot if dense else ranks[slot]

        @pl.when(held[slot] == 1)
        def _():
            pltpu.make_async_copy(recv_ref.at[unit], held_ref.at[slot], in_sem.at[slot]).start()

    for slot in range(per_device):
        limit = limits[slot] - start

        @pl.when(limit > 0)
        def _():
            pltpu.make_async_copy(recv_ref.at[0], held_ref.at[slot], in_sem.at[slot]).wait()

        @pl.when(limit <= 0)
        def _():
            held_ref[slot] = jnp.zeros_like(held_ref[slot])

        @pl.when((limit >= 0) & (limit < rows))
        def _():
            row = lax.broadcasted_iota(jnp.int32, (rows, head_dim), 0)
            for part in range(2):
                fresh = token_ref[slot, group + part : group + part + 1, :].astype(jnp.float32)
                block = held_ref[slot, part].astype(jnp.float32)
                block = jnp.where(row < limit, block, jnp.where(row == limit, fresh, 0.0))
                held_ref[slot, part] = block.astype(held_ref.dtype)

        for part in range(2):
            pltpu.make_async_copy(
                held_ref.at[slot, part],
                cache_ref.at[part, slot, pl.ds(pl.multiple_of(start, rows), rows)],
                out_sem.at[slot, part],
            ).start()

    outputs = []
    for slot in range(per_device):
        limit = limits[slot] - start
        if first:
            old_max = jnp.full((group, head_dim), NEG_FILL, jnp.float32)
            old_sum = jnp.zeros((group, head_dim), jnp.float32)
            old_out = jnp.zeros((group, head_dim), jnp.float32)
        else:
            old_max, old_sum, old_out = old_ref[0, slot], old_ref[1, slot], old_ref[2, slot]
        query = token_ref[slot, :group, :]
        scores = lax.dot_general(
            query, held_ref[slot, 0], (((1,), (1,)), ((), ())), preferred_element_type=jnp.float32
        )
        scores = scores * scale
        visible = lax.broadcasted_iota(jnp.int32, scores.shape, 1) <= limit
        scores = jnp.where(visible, scores, NEG_FILL)
        new_max = jnp.maximum(old_max, jnp.max(scores, axis=1, keepdims=True))
        weights = jnp.where(visible, jnp.exp(scores - new_max[:, :1]), 0.0)
        factor = jnp.exp(old_max - new_max)
        high = weights.astype(jnp.bfloat16)
        rest = weights - high.astype(jnp.float32)
        middle = rest.astype(jnp.bfloat16)
        low = (rest - middle.astype(jnp.float32)).astype(jnp.bfloat16)
        value = held_ref[slot, 1]
        summed = sum(
            jnp.dot(term, value, preferred_element_type=jnp.float32) for term in (low, middle, high)
        )
        new_sum = old_sum * factor + jnp.sum(weights, axis=1, keepdims=True)
        new_out = old_out * factor + summed
        if last:
            mean = new_out / new_sum
            heads = [mean[head : head + 1] for head in range(group)]
            outputs.append(jnp.concatenate(heads, axis=1))
        else:
            state_ref[0, slot] = new_max
            state_ref[1, slot] = new_sum
            state_ref[2, slot] = new_out
    if last:
        state_ref[...] = jnp.concatenate(outputs, axis=0).astype(state_ref.dtype)

    for slot in range(per_device):
        for part in range(2):
            pltpu.make_async_copy(
                held_ref.at[slot, part],
                cache_ref.at[part, slot, pl.ds(pl.multiple_of(start, rows), rows)],
                out_sem.at[slot, part],
            ).wait()


def absorb(scalars, recv, tokens, carry, offset, head_count, devices, dense, last):
    per_device, _, rows, head_dim = recv.shape
    group = tokens.shape[1] - 2
    first = carry is None
    anywhere, whole = pl.BlockSpec(memory_space=pl.ANY), pl.BlockSpec(memory_space=pltpu.VMEM)
    dtype = recv.dtype
    return pl.pallas_call(
        functools.partial(
            absorb_body, offset, per_device, head_count, 1.0 / math.sqrt(head_dim), dense, first, last
        ),
        out_shape=[
            jax.ShapeDtypeStruct((2, per_device, rows * devices, head_dim), dtype),
            jax.ShapeDtypeStruct((per_device, group * head_dim), dtype)
            if last
            else jax.ShapeDtypeStruct((3, per_device, group, head_dim), jnp.float32),
        ],
        grid_spec=pltpu.PrefetchScalarGridSpec(
            num_scalar_prefetch=3,
            grid=(1,),
            in_specs=[anywhere, whole] + ([] if first else [anywhere, whole]),
            out_specs=[anywhere, whole],
            scratch_shapes=[
                pltpu.VMEM((per_device, 2, rows, head_dim), dtype),
                pltpu.SemaphoreType.DMA((per_device,)),
                pltpu.SemaphoreType.DMA((per_device, 2)),
            ],
        ),
        input_output_aliases={} if first else {5: 0} if last else {5: 0, 6: 1},
        cost_estimate=pl.CostEstimate(
            flops=per_device * 8 * group * rows * head_dim * 16,
            bytes_accessed=4 * per_device * 2 * rows * head_dim,
            transcendentals=per_device * group * rows,
        ),
        name="absorb",
    )(*scalars, recv, tokens, *(() if first else carry))


def local(kv_prefill, queries, fresh_kv, lengths, decode_slot_pair):
    devices = lax.axis_size("wide")
    seq_count, head_count, local_len, head_dim = kv_prefill.shape[1:]
    item_count = seq_count * head_count
    per_device = item_count // devices
    group_size = queries.shape[1] // head_dim
    rank = lax.axis_index("wide").astype(jnp.int32)
    kv = kv_prefill.reshape(2, item_count, local_len, head_dim)
    scalars = (rank.reshape(1), decode_slot_pair, lengths)

    def pairs_of(offset):
        return [(device, device ^ offset) for device in range(devices)]

    def go_round(tokens, stride, steps):
        blocks = [
            lax.ppermute(tokens, "wide", pairs_of(step * stride)) for step in range(1, steps)
        ]
        return jnp.concatenate([tokens, *blocks], axis=0)

    half = devices // 2
    quarter = max(half // 2, 1)
    near = [*range(quarter, half), *range(1, quarter)]
    far = [*range(half, devices)]
    arrived = {}
    dense = {offset: True for offset in range(devices)}
    order = [
        *(offset for both in zip(far[:quarter], near[:quarter]) for offset in both),
        *near[quarter:],
        *far[quarter:],
    ]
    early = 1
    for offset in order[:early]:
        units = gather_units(scalars, kv, offset, per_device, head_count, True)
        arrived[offset] = lax.ppermute(units, "wide", pairs_of(offset))
    units, queries, fresh_kv = lax.optimization_barrier((units, queries, fresh_kv))
    tokens = jnp.concatenate(
        [queries.reshape(per_device, group_size, head_dim), jnp.swapaxes(fresh_kv, 0, 1)], axis=1
    )
    stride = min(4, devices)
    tokens = go_round(tokens, 1, stride)
    while stride < devices:
        steps = min(4, devices // stride)
        tokens = go_round(tokens, stride, steps)
        stride *= steps
    for offset in order[early:]:
        units = gather_units(scalars, kv, offset, per_device, head_count, True)
        arrived[offset] = lax.ppermute(units, "wide", pairs_of(offset))
    arrived[0] = gather_units(scalars, kv, 0, per_device, head_count, True)
    own_slots = lax.dynamic_slice_in_dim(decode_slot_pair, rank * per_device, per_device)
    rows = ((own_slots // per_device) ^ rank) * per_device + own_slots % per_device
    own_tokens = jnp.take(tokens, rows, axis=0)

    carry = None
    for offset in [0, *order]:
        carry = absorb(
            scalars,
            arrived[offset],
            own_tokens,
            carry,
            offset,
            head_count,
            devices,
            dense[offset],
            offset == order[-1],
        )
    return tuple(carry)


def solution(mesh):
    in_specs = (
        P(None, "grp", None, "wide", None),
        P(("grp", "wide"), None),
        P(None, ("grp", "wide"), None),
        P("grp"),
        P("grp"),
    )
    out_specs = (P(None, ("grp", "wide"), None, None), P(("grp", "wide"), None))

    return jax.shard_map(local, mesh=mesh, in_specs=in_specs, out_specs=out_specs, check_vma=False)
```

profile of v0, /device:TPU:9, one launch (start us, length us, event | category | flops | bytes accessed | tf_op | source)
XLA Modules:
  0.0 389.3 jit_solution(4218903821873306213)
XLA Ops:
  0.7 2.8 gather_units.17
  3.5 0.6 constant_dynamic-update-slice_fusion.1
  4.1 0.6 constant_dynamic-update-slice_fusion
  4.7 0.7 collective-permute-start.1
  5.3 1.2 collective-permute-start.2
  7.0 1.0 collective-permute-done.2
  7.9 1.8 collective-permute-done.3
  10.0 2.3 collective-permute-start.20
  12.3 2.7 gather_units.30
  15.0 1.4 collective-permute-start.19
  16.3 2.7 gather_units.29
  19.0 1.1 collective-permute-start.18
  20.2 2.7 gather_units.28
  23.1 2.3 collective-permute-start.5
  25.3 79.9 %collective-permute-done.5 = bf16[16,10,128]{2,1,0:T(8,128)(2,1)S(1)} collective-permute-done((bf16[16,10,128]{2,1,0:T(8,128)(2,1)S(1)}, bf16[16,10,128]{2,1,0:T(8,128)(2,1)S(1)}, u32[]{:S(2)}, u32[]{:S(2)}) %collective-permute-start.5) | collective-permute-done | bytes 40992 | tf_op jit(solution)/shard_map/ppermute | solution.py:227
  105.2 1.1 collective-permute-start.6
  106.3 2.7 gather_units.27
  109.0 2.5 collective-permute-start.16
  111.6 2.7 gather_units.26
  114.3 2.7 gather_units.25
  116.9 2.7 gather_units.24
  119.6 2.7 gather_units.23
  122.4 6.6 %collective-permute-start.14 = (bf16[4,2,512,128]{3,2,1,0:T(8,128)(2,1)}, bf16[4,2,512,128]{3,2,1,0:T(8,128)(2,1)}, u32[]{:S(2)}, u32[]{:S(2)}) collective-permute-start(bf16[4,2,512,128]{3,2,1,0:T(8,128)(2,1)} %gather_units.25), channel_id=1, source_target_pairs={{0,11},{1,10},{2,9},{3,8},{4,15},{5,14},{6,13},{7,12},{8,3},{9,2},... | collective-permute-start | bytes 3145736 | tf_op jit(solution)/shard_map/ppermute | solution.py:258
  129.2 2.7 gather_units.22
  131.9 27.1 %collective-permute-done.16.recv_ref = bf16[4,2,512,128]{3,2,1,0:T(8,128)(2,1)} collective-permute-done((bf16[4,2,512,128]{3,2,1,0:T(8,128)(2,1)}, bf16[4,2,512,128]{3,2,1,0:T(8,128)(2,1)}, u32[]{:S(2)}, u32[]{:S(2)}) %collective-permute-start.16) | collective-permute-done | bytes 1048608 | tf_op jit(solution)/shard_map/ppermute | solution.py:258
  159.2 2.7 gather_units.31.recv_ref
  161.9 2.7 gather_units.21
  164.6 2.7 gather_units.20
  167.3 2.7 gather_units.19
  170.0 2.8 gather_units.18
  172.8 2.8 gather_units.16
  175.8 0.6 constant_dynamic-update-slice_fusion.7
  176.4 2.3 collective-permute-start.10
  178.7 23.2 %collective-permute-done.14.recv_ref = bf16[4,2,512,128]{3,2,1,0:T(8,128)(2,1)} collective-permute-done((bf16[4,2,512,128]{3,2,1,0:T(8,128)(2,1)}, bf16[4,2,512,128]{3,2,1,0:T(8,128)(2,1)}, u32[]{:S(2)}, u32[]{:S(2)}) %collective-permute-start.14) | collective-permute-done | bytes 1048608 | tf_op jit(solution)/shard_map/ppermute | solution.py:258
  202.3 28.9 %collective-permute-done.13.recv_ref = bf16[4,2,512,128]{3,2,1,0:T(8,128)(2,1)} collective-permute-done((bf16[4,2,512,128]{3,2,1,0:T(8,128)(2,1)}, bf16[4,2,512,128]{3,2,1,0:T(8,128)(2,1)}, u32[]{:S(2)}, u32[]{:S(2)}) %collective-permute-start.13) | collective-permute-done | bytes 1048608 | tf_op jit(solution)/shard_map/ppermute | solution.py:258
  231.2 5.7 %collective-permute-start.8 = (bf16[4,2,512,128]{3,2,1,0:T(8,128)(2,1)S(1)}, bf16[4,2,512,128]{3,2,1,0:T(8,128)(2,1)}, u32[]{:S(2)}, u32[]{:S(2)}) collective-permute-start(bf16[4,2,512,128]{3,2,1,0:T(8,128)(2,1)S(1)} %copy-done.4), channel_id=1, source_target_pairs={{0,13},{1,12},{2,15},{3,14},{4,9},{5,8},{6,11},{7,10},{8,5},{9,4},... | collective-permute-start | bytes 3145736 | tf_op jit(solution)/shard_map/ppermute | solution.py:258
  236.9 1.4 collective-permute-start.7
  238.3 0.6 constant_dynamic-update-slice_fusion.6
  239.1 0.6 constant_dynamic-update-slice_fusion.5
  239.7 0.6 constant_dynamic-update-slice_fusion.4
  240.4 0.6 constant_dynamic-update-slice_fusion.3
  241.0 0.6 constant_dynamic-update-slice_fusion.2
  241.6 1.5 gather_fusion
  243.1 0.7 broadcast_select_fusion.refs_0_
  243.8 4.5 %absorb.16 = (bf16[2,4,8192,128]{3,2,1,0:T(8,128)(2,1)}, f32[3,4,8,128]{3,2,1,0:T(8,128)}) custom-call(s32[1]{0:T(128)} %bitcast.me_ref, s32[64]{0:T(128)} %slots_ref.63, s32[8]{0:T(128)} %lengths_ref.63, bf16[4,2,512,128]{3,2,1,0:T(8,128)(2,1)} %gather_units.31.recv_ref, bf16[4,10,128]{2,1,0:T(8,128)(2,1)} %broadcast_select_fusion.refs_0_), custom_call_target="tpu_custom_call" | custom-call | flops 268435456 | bytes 2097152 | tf_op jit(solution)/shard_map/absorb/pallas_call | solution.py:181
  248.3 5.0 %absorb.17 = (bf16[2,4,8192,128]{3,2,1,0:T(8,128)(2,1)}, f32[3,4,8,128]{3,2,1,0:T(8,128)}) custom-call(s32[1]{0:T(128)} %bitcast.me_ref, s32[64]{0:T(128)} %slots_ref.63, s32[8]{0:T(128)} %lengths_ref.63, bf16[4,2,512,128]{3,2,1,0:T(8,128)(2,1)} %collective-permute-done.20.recv_ref, ...), custom_call_target="tpu_custom_call", output_to_operand_aliasing={{0}: (5, {}), {1}: (6, {})} | custom-call | flops 268435456 | bytes 2097152 | tf_op jit(solution)/shard_map/absorb/pallas_call | solution.py:181
  253.3 4.9 %absorb.18 = (bf16[2,4,8192,128]{3,2,1,0:T(8,128)(2,1)}, f32[3,4,8,128]{3,2,1,0:T(8,128)}) custom-call(s32[1]{0:T(128)} %bitcast.me_ref, s32[64]{0:T(128)} %slots_ref.63, s32[8]{0:T(128)} %lengths_ref.63, bf16[4,2,512,128]{3,2,1,0:T(8,128)(2,1)} %copy-done.2, ...), custom_call_target="tpu_custom_call", output_to_operand_aliasing={{0}: (5, {}), {1}: (6, {})} | custom-call | flops 268435456 | bytes 2097152 | tf_op jit(solution)/shard_map/absorb/pallas_call | solution.py:181
  258.2 4.9 %absorb.19 = (bf16[2,4,8192,128]{3,2,1,0:T(8,128)(2,1)}, f32[3,4,8,128]{3,2,1,0:T(8,128)}) custom-call(s32[1]{0:T(128)} %bitcast.me_ref, s32[64]{0:T(128)} %slots_ref.63, s32[8]{0:T(128)} %lengths_ref.63, bf16[4,2,512,128]{3,2,1,0:T(8,128)(2,1)} %copy-done.1, ...), custom_call_target="tpu_custom_call", output_to_operand_aliasing={{0}: (5, {}), {1}: (6, {})} | custom-call | flops 268435456 | bytes 2097152 | tf_op jit(solution)/shard_map/absorb/pallas_call | solution.py:181
  263.1 4.9 %absorb.20 = (bf16[2,4,8192,128]{3,2,1,0:T(8,128)(2,1)}, f32[3,4,8,128]{3,2,1,0:T(8,128)}) custom-call(s32[1]{0:T(128)} %bitcast.me_ref, s32[64]{0:T(128)} %slots_ref.63, s32[8]{0:T(128)} %lengths_ref.63, bf16[4,2,512,128]{3,2,1,0:T(8,128)(2,1)} %copy-done, ...), custom_call_target="tpu_custom_call", output_to_operand_aliasing={{0}: (5, {}), {1}: (6, {})} | custom-call | flops 268435456 | bytes 2097152 | tf_op jit(solution)/shard_map/absorb/pallas_call | solution.py:181
  268.1 5.1 %absorb.21 = (bf16[2,4,8192,128]{3,2,1,0:T(8,128)(2,1)}, f32[3,4,8,128]{3,2,1,0:T(8,128)}) custom-call(s32[1]{0:T(128)} %bitcast.me_ref, s32[64]{0:T(128)} %slots_ref.63, s32[8]{0:T(128)} %lengths_ref.63, bf16[4,2,512,128]{3,2,1,0:T(8,128)(2,1)} %collective-permute-done.16.recv_ref, ...), custom_call_target="tpu_custom_call", output_to_operand_aliasing={{0}: (5, {}), {1}: (6, {})} | custom-call | flops 268435456 | bytes 2097152 | tf_op jit(solution)/shard_map/absorb/pallas_call | solution.py:181
  273.2 4.9 %absorb.22 = (bf16[2,4,8192,128]{3,2,1,0:T(8,128)(2,1)}, f32[3,4,8,128]{3,2,1,0:T(8,128)}) custom-call(s32[1]{0:T(128)} %bitcast.me_ref, s32[64]{0:T(128)} %slots_ref.63, s32[8]{0:T(128)} %lengths_ref.63, bf16[4,2,512,128]{3,2,1,0:T(8,128)(2,1)} %collective-permute-done.15.recv_ref, ...), custom_call_target="tpu_custom_call", output_to_operand_aliasing={{0}: (5, {}), {1}: (6, {})} | custom-call | flops 268435456 | bytes 2097152 | tf_op jit(solution)/shard_map/absorb/pallas_call | solution.py:181
  278.1 5.0 %absorb.23 = (bf16[2,4,8192,128]{3,2,1,0:T(8,128)(2,1)}, f32[3,4,8,128]{3,2,1,0:T(8,128)}) custom-call(s32[1]{0:T(128)} %bitcast.me_ref, s32[64]{0:T(128)} %slots_ref.63, s32[8]{0:T(128)} %lengths_ref.63, bf16[4,2,512,128]{3,2,1,0:T(8,128)(2,1)} %collective-permute-done.14.recv_ref, ...), custom_call_target="tpu_custom_call", output_to_operand_aliasing={{0}: (5, {}), {1}: (6, {})} | custom-call | flops 268435456 | bytes 2097152 | tf_op jit(solution)/shard_map/absorb/pallas_call | solution.py:181
  283.1 4.9 %absorb.24 = (bf16[2,4,8192,128]{3,2,1,0:T(8,128)(2,1)}, f32[3,4,8,128]{3,2,1,0:T(8,128)}) custom-call(s32[1]{0:T(128)} %bitcast.me_ref, s32[64]{0:T(128)} %slots_ref.63, s32[8]{0:T(128)} %lengths_ref.63, bf16[4,2,512,128]{3,2,1,0:T(8,128)(2,1)} %collective-permute-done.13.recv_ref, ...), custom_call_target="tpu_custom_call", output_to_operand_aliasing={{0}: (5, {}), {1}: (6, {})} | custom-call | flops 268435456 | bytes 2097152 | tf_op jit(solution)/shard_map/absorb/pallas_call | solution.py:181
  288.0 4.9 %absorb.25 = (bf16[2,4,8192,128]{3,2,1,0:T(8,128)(2,1)}, f32[3,4,8,128]{3,2,1,0:T(8,128)}) custom-call(s32[1]{0:T(128)} %bitcast.me_ref, s32[64]{0:T(128)} %slots_ref.63, s32[8]{0:T(128)} %lengths_ref.63, bf16[4,2,512,128]{3,2,1,0:T(8,128)(2,1)} %collective-permute-done.12.recv_ref, ...), custom_call_target="tpu_custom_call", output_to_operand_aliasing={{0}: (5, {}), {1}: (6, {})} | custom-call | flops 268435456 | bytes 2097152 | tf_op jit(solution)/shard_map/absorb/pallas_call | solution.py:181
  292.9 4.9 %absorb.26 = (bf16[2,4,8192,128]{3,2,1,0:T(8,128)(2,1)}, f32[3,4,8,128]{3,2,1,0:T(8,128)}) custom-call(s32[1]{0:T(128)} %bitcast.me_ref, s32[64]{0:T(128)} %slots_ref.63, s32[8]{0:T(128)} %lengths_ref.63, bf16[4,2,512,128]{3,2,1,0:T(8,128)(2,1)} %collective-permute-done.11.recv_ref, ...), custom_call_target="tpu_custom_call", output_to_operand_aliasing={{0}: (5, {}), {1}: (6, {})} | custom-call | flops 268435456 | bytes 2097152 | tf_op jit(solution)/shard_map/absorb/pallas_call | solution.py:181
  297.9 4.9 %absorb.27 = (bf16[2,4,8192,128]{3,2,1,0:T(8,128)(2,1)}, f32[3,4,8,128]{3,2,1,0:T(8,128)}) custom-call(s32[1]{0:T(128)} %bitcast.me_ref, s32[64]{0:T(128)} %slots_ref.63, s32[8]{0:T(128)} %lengths_ref.63, bf16[4,2,512,128]{3,2,1,0:T(8,128)(2,1)} %collective-permute-done.10.recv_ref, ...), custom_call_target="tpu_custom_call", output_to_operand_aliasing={{0}: (5, {}), {1}: (6, {})} | custom-call | flops 268435456 | bytes 2097152 | tf_op jit(solution)/shard_map/absorb/pallas_call | solution.py:181
  302.8 13.3 %collective-permute-done.9.recv_ref = bf16[4,2,512,128]{3,2,1,0:T(8,128)(2,1)} collective-permute-done((bf16[4,2,512,128]{3,2,1,0:T(8,128)(2,1)S(1)}, bf16[4,2,512,128]{3,2,1,0:T(8,128)(2,1)}, u32[]{:S(2)}, u32[]{:S(2)}) %collective-permute-start.9) | collective-permute-done | bytes 1048608 | tf_op jit(solution)/shard_map/ppermute | solution.py:258
  316.1 4.9 %absorb.28 = (bf16[2,4,8192,128]{3,2,1,0:T(8,128)(2,1)}, f32[3,4,8,128]{3,2,1,0:T(8,128)}) custom-call(s32[1]{0:T(128)} %bitcast.me_ref, s32[64]{0:T(128)} %slots_ref.63, s32[8]{0:T(128)} %lengths_ref.63, bf16[4,2,512,128]{3,2,1,0:T(8,128)(2,1)} %collective-permute-done.9.recv_ref, ...), custom_call_target="tpu_custom_call", output_to_operand_aliasing={{0}: (5, {}), {1}: (6, {})} | custom-call | flops 268435456 | bytes 2097152 | tf_op jit(solution)/shard_map/absorb/pallas_call | solution.py:181
  321.0 19.2 %collective-permute-done.8.recv_ref = bf16[4,2,512,128]{3,2,1,0:T(8,128)(2,1)} collective-permute-done((bf16[4,2,512,128]{3,2,1,0:T(8,128)(2,1)S(1)}, bf16[4,2,512,128]{3,2,1,0:T(8,128)(2,1)}, u32[]{:S(2)}, u32[]{:S(2)}) %collective-permute-start.8) | collective-permute-done | bytes 1048608 | tf_op jit(solution)/shard_map/ppermute | solution.py:258
  340.2 4.9 %absorb.29 = (bf16[2,4,8192,128]{3,2,1,0:T(8,128)(2,1)}, f32[3,4,8,128]{3,2,1,0:T(8,128)}) custom-call(s32[1]{0:T(128)} %bitcast.me_ref, s32[64]{0:T(128)} %slots_ref.63, s32[8]{0:T(128)} %lengths_ref.63, bf16[4,2,512,128]{3,2,1,0:T(8,128)(2,1)} %collective-permute-done.8.recv_ref, ...), custom_call_target="tpu_custom_call", output_to_operand_aliasing={{0}: (5, {}), {1}: (6, {})} | custom-call | flops 268435456 | bytes 2097152 | tf_op jit(solution)/shard_map/absorb/pallas_call | solution.py:181
  345.1 16.0 %collective-permute-done.7.recv_ref = bf16[4,2,512,128]{3,2,1,0:T(8,128)(2,1)} collective-permute-done((bf16[4,2,512,128]{3,2,1,0:T(8,128)(2,1)S(1)}, bf16[4,2,512,128]{3,2,1,0:T(8,128)(2,1)}, u32[]{:S(2)}, u32[]{:S(2)}) %collective-permute-start.7) | collective-permute-done | bytes 1048608 | tf_op jit(solution)/shard_map/ppermute | solution.py:258
  361.1 4.9 %absorb.30 = (bf16[2,4,8192,128]{3,2,1,0:T(8,128)(2,1)}, f32[3,4,8,128]{3,2,1,0:T(8,128)}) custom-call(s32[1]{0:T(128)} %bitcast.me_ref, s32[64]{0:T(128)} %slots_ref.63, s32[8]{0:T(128)} %lengths_ref.63, bf16[4,2,512,128]{3,2,1,0:T(8,128)(2,1)} %collective-permute-done.7.recv_ref, ...), custom_call_target="tpu_custom_call", output_to_operand_aliasing={{0}: (5, {}), {1}: (6, {})} | custom-call | flops 268435456 | bytes 2097152 | tf_op jit(solution)/shard_map/absorb/pallas_call | solution.py:181
  366.0 18.2 %collective-permute-done.recv_ref = bf16[4,2,512,128]{3,2,1,0:T(8,128)(2,1)} collective-permute-done((bf16[4,2,512,128]{3,2,1,0:T(8,128)(2,1)}, bf16[4,2,512,128]{3,2,1,0:T(8,128)(2,1)}, u32[]{:S(2)}, u32[]{:S(2)}) %collective-permute-start) | collective-permute-done | bytes 1048608 | tf_op jit(solution)/shard_map/ppermute | solution.py:258
  384.2 4.9 %absorb.31 = (bf16[2,4,8192,128]{3,2,1,0:T(8,128)(2,1)}, bf16[4,1024]{1,0:T(4,128)(2,1)}) custom-call(s32[1]{0:T(128)} %bitcast.me_ref, s32[64]{0:T(128)} %slots_ref.63, s32[8]{0:T(128)} %lengths_ref.63, bf16[4,2,512,128]{3,2,1,0:T(8,128)(2,1)} %collective-permute-done.recv_ref, ...), custom_call_target="tpu_custom_call", output_to_operand_aliasing={{0}: (5, {})} | custom-call | flops 268435456 | bytes 2097152 | tf_op jit(solution)/shard_map/absorb/pallas_call | solution.py:181
  (41 shorter events, 2.3 us)
Async XLA Ops:
  0.6 2.8 copy-start.7
  0.6 3.4 copy-start.8
  4.7 2.3 collective-permute-start.1
  5.3 2.6 collective-permute-start.2
  6.6 3.2 collective-permute-start.3
  9.8 13.3 %collective-permute-start.4 = (bf16[16,10,128]{2,1,0:T(8,128)(2,1)S(1)}, bf16[16,10,128]{2,1,0:T(8,128)(2,1)S(1)}, u32[]{:S(2)}, u32[]{:S(2)}) collective-permute-start(bf16[16,10,128]{2,1,0:T(8,128)(2,1)S(1)} %pad_maximum_fusion), channel_id=1, source_target_pairs={{0,4},{1,5},{2,6},{3,7},{4,0},{5,1},{6,2},{7,3},{8,12},{9,13},{10,... | collective-permute-start | bytes 122888 | tf_op jit(solution)/shard_map/ppermute | solution.py:227
  10.0 112.3 %collective-permute-start.20 = (bf16[4,2,512,128]{3,2,1,0:T(8,128)(2,1)}, bf16[4,2,512,128]{3,2,1,0:T(8,128)(2,1)}, u32[]{:S(2)}, u32[]{:S(2)}) collective-permute-start(bf16[4,2,512,128]{3,2,1,0:T(8,128)(2,1)} %gather_units.17), channel_id=1, source_target_pairs={{0,8},{1,9},{2,10},{3,11},{4,12},{5,13},{6,14},{7,15},{8,0},{9,1},... | collective-permute-start | bytes 3145736 | tf_op jit(solution)/shard_map/ppermute | solution.py:245
  15.0 107.4 %collective-permute-start.19 = (bf16[4,2,512,128]{3,2,1,0:T(8,128)(2,1)}, bf16[4,2,512,128]{3,2,1,0:T(8,128)(2,1)S(1)}, u32[]{:S(2)}, u32[]{:S(2)}) collective-permute-start(bf16[4,2,512,128]{3,2,1,0:T(8,128)(2,1)} %gather_units.30), channel_id=1, source_target_pairs={{0,4},{1,5},{2,6},{3,7},{4,0},{5,1},{6,2},{7,3},{8,12},{9,13},{10,... | collective-permute-start | bytes 3145736 | tf_op jit(solution)/shard_map/ppermute | solution.py:258
  19.0 109.9 %collective-permute-start.18 = (bf16[4,2,512,128]{3,2,1,0:T(8,128)(2,1)}, bf16[4,2,512,128]{3,2,1,0:T(8,128)(2,1)S(1)}, u32[]{:S(2)}, u32[]{:S(2)}) collective-permute-start(bf16[4,2,512,128]{3,2,1,0:T(8,128)(2,1)} %gather_units.29), channel_id=1, source_target_pairs={{0,9},{1,8},{2,11},{3,10},{4,13},{5,12},{6,15},{7,14},{8,1},{9,0},... | collective-permute-start | bytes 3145736 | tf_op jit(solution)/shard_map/ppermute | solution.py:258
  22.9 106.2 %collective-permute-start.17 = (bf16[4,2,512,128]{3,2,1,0:T(8,128)(2,1)}, bf16[4,2,512,128]{3,2,1,0:T(8,128)(2,1)S(1)}, u32[]{:S(2)}, u32[]{:S(2)}) collective-permute-start(bf16[4,2,512,128]{3,2,1,0:T(8,128)(2,1)} %gather_units.28), channel_id=1, source_target_pairs={{0,5},{1,4},{2,7},{3,6},{4,1},{5,0},{6,3},{7,2},{8,13},{9,12},{10,... | collective-permute-start | bytes 3145736 | tf_op jit(solution)/shard_map/ppermute | solution.py:258
  23.1 82.2 %collective-permute-start.5 = (bf16[16,10,128]{2,1,0:T(8,128)(2,1)S(1)}, bf16[16,10,128]{2,1,0:T(8,128)(2,1)S(1)}, u32[]{:S(2)}, u32[]{:S(2)}) collective-permute-start(bf16[16,10,128]{2,1,0:T(8,128)(2,1)S(1)} %pad_maximum_fusion), channel_id=1, source_target_pairs={{0,8},{1,9},{2,10},{3,11},{4,12},{5,13},{6,14},{7,15},{8,0},{9,1},... | collective-permute-start | bytes 122888 | tf_op jit(solution)/shard_map/ppermute | solution.py:227
  105.2 3.8 collective-permute-start.6
  109.0 49.9 %collective-permute-start.16 = (bf16[4,2,512,128]{3,2,1,0:T(8,128)(2,1)}, bf16[4,2,512,128]{3,2,1,0:T(8,128)(2,1)}, u32[]{:S(2)}, u32[]{:S(2)}) collective-permute-start(bf16[4,2,512,128]{3,2,1,0:T(8,128)(2,1)} %gather_units.27), channel_id=1, source_target_pairs={{0,10},{1,11},{2,8},{3,9},{4,14},{5,15},{6,12},{7,13},{8,2},{9,3},... | collective-permute-start | bytes 3145736 | tf_op jit(solution)/shard_map/ppermute | solution.py:258
  122.3 54.1 %collective-permute-start.15 = (bf16[4,2,512,128]{3,2,1,0:T(8,128)(2,1)}, bf16[4,2,512,128]{3,2,1,0:T(8,128)(2,1)}, u32[]{:S(2)}, u32[]{:S(2)}) collective-permute-start(bf16[4,2,512,128]{3,2,1,0:T(8,128)(2,1)} %gather_units.26), channel_id=1, source_target_pairs={{0,6},{1,7},{2,4},{3,5},{4,2},{5,3},{6,0},{7,1},{8,14},{9,15},{10,... | collective-permute-start | bytes 3145736 | tf_op jit(solution)/shard_map/ppermute | solution.py:258
  122.4 39.5 %copy-start.2 = (bf16[4,2,512,128]{3,2,1,0:T(8,128)(2,1)}, bf16[4,2,512,128]{3,2,1,0:T(8,128)(2,1)S(1)}, u32[]{:S(2)}) copy-start(bf16[4,2,512,128]{3,2,1,0:T(8,128)(2,1)S(1)} %collective-permute-done.19.recv_ref) | copy-start | bytes 3145732
  122.4 79.5 %collective-permute-start.14 = (bf16[4,2,512,128]{3,2,1,0:T(8,128)(2,1)}, bf16[4,2,512,128]{3,2,1,0:T(8,128)(2,1)}, u32[]{:S(2)}, u32[]{:S(2)}) collective-permute-start(bf16[4,2,512,128]{3,2,1,0:T(8,128)(2,1)} %gather_units.25), channel_id=1, source_target_pairs={{0,11},{1,10},{2,9},{3,8},{4,15},{5,14},{6,13},{7,12},{8,3},{9,2},... | collective-permute-start | bytes 3145736 | tf_op jit(solution)/shard_map/ppermute | solution.py:258
  129.0 32.9 %copy-start.1 = (bf16[4,2,512,128]{3,2,1,0:T(8,128)(2,1)}, bf16[4,2,512,128]{3,2,1,0:T(8,128)(2,1)S(1)}, u32[]{:S(2)}) copy-start(bf16[4,2,512,128]{3,2,1,0:T(8,128)(2,1)S(1)} %collective-permute-done.18.recv_ref) | copy-start | bytes 3145732
  129.0 102.2 %collective-permute-start.13 = (bf16[4,2,512,128]{3,2,1,0:T(8,128)(2,1)}, bf16[4,2,512,128]{3,2,1,0:T(8,128)(2,1)}, u32[]{:S(2)}, u32[]{:S(2)}) collective-permute-start(bf16[4,2,512,128]{3,2,1,0:T(8,128)(2,1)} %gather_units.24), channel_id=1, source_target_pairs={{0,7},{1,6},{2,5},{3,4},{4,3},{5,2},{6,1},{7,0},{8,15},{9,14},{10,... | collective-permute-start | bytes 3145736 | tf_op jit(solution)/shard_map/ppermute | solution.py:258
  129.1 32.8 %copy-start = (bf16[4,2,512,128]{3,2,1,0:T(8,128)(2,1)}, bf16[4,2,512,128]{3,2,1,0:T(8,128)(2,1)S(1)}, u32[]{:S(2)}) copy-start(bf16[4,2,512,128]{3,2,1,0:T(8,128)(2,1)S(1)} %collective-permute-done.17.recv_ref) | copy-start | bytes 3145732
  129.1 107.8 %collective-permute-start.12 = (bf16[4,2,512,128]{3,2,1,0:T(8,128)(2,1)}, bf16[4,2,512,128]{3,2,1,0:T(8,128)(2,1)}, u32[]{:S(2)}, u32[]{:S(2)}) collective-permute-start(bf16[4,2,512,128]{3,2,1,0:T(8,128)(2,1)} %gather_units.23), channel_id=1, source_target_pairs={{0,1},{1,0},{2,3},{3,2},{4,5},{5,4},{6,7},{7,6},{8,9},{9,8},{10,11... | collective-permute-start | bytes 3145736 | tf_op jit(solution)/shard_map/ppermute | solution.py:258
  158.9 79.9 %collective-permute-start.11 = (bf16[4,2,512,128]{3,2,1,0:T(8,128)(2,1)}, bf16[4,2,512,128]{3,2,1,0:T(8,128)(2,1)}, u32[]{:S(2)}, u32[]{:S(2)}) collective-permute-start(bf16[4,2,512,128]{3,2,1,0:T(8,128)(2,1)} %gather_units.22), channel_id=1, source_target_pairs={{0,2},{1,3},{2,0},{3,1},{4,6},{5,7},{6,4},{7,5},{8,10},{9,11},{10,... | collective-permute-start | bytes 3145736 | tf_op jit(solution)/shard_map/ppermute | solution.py:258
  170.0 5.7 %copy-start.6 = (s32[64]{0:T(128)S(1)}, s32[64]{0:T(128)}, u32[]{:S(2)}) copy-start(s32[64]{0:T(128)} %slots_ref.63) | copy-start | bytes 772
  170.0 31.9 %copy-start.5 = (bf16[4,2,512,128]{3,2,1,0:T(8,128)(2,1)S(1)}, bf16[4,2,512,128]{3,2,1,0:T(8,128)(2,1)}, u32[]{:S(2)}) copy-start(bf16[4,2,512,128]{3,2,1,0:T(8,128)(2,1)} %gather_units.20) | copy-start | bytes 3145732
  170.0 61.2 %copy-start.4 = (bf16[4,2,512,128]{3,2,1,0:T(8,128)(2,1)S(1)}, bf16[4,2,512,128]{3,2,1,0:T(8,128)(2,1)}, u32[]{:S(2)}) copy-start(bf16[4,2,512,128]{3,2,1,0:T(8,128)(2,1)} %gather_units.19) | copy-start | bytes 3145732
  172.8 64.1 %copy-start.3 = (bf16[4,2,512,128]{3,2,1,0:T(8,128)(2,1)S(1)}, bf16[4,2,512,128]{3,2,1,0:T(8,128)(2,1)}, u32[]{:S(2)}) copy-start(bf16[4,2,512,128]{3,2,1,0:T(8,128)(2,1)} %gather_units.18) | copy-start | bytes 3145732
  176.4 121.5 %collective-permute-start.10 = (bf16[4,2,512,128]{3,2,1,0:T(8,128)(2,1)}, bf16[4,2,512,128]{3,2,1,0:T(8,128)(2,1)}, u32[]{:S(2)}, u32[]{:S(2)}) collective-permute-start(bf16[4,2,512,128]{3,2,1,0:T(8,128)(2,1)} %gather_units.21), channel_id=1, source_target_pairs={{0,3},{1,2},{2,1},{3,0},{4,7},{5,6},{6,5},{7,4},{8,11},{9,10},{10,... | collective-permute-start | bytes 3145736 | tf_op jit(solution)/shard_map/ppermute | solution.py:258
  201.9 114.2 %collective-permute-start.9 = (bf16[4,2,512,128]{3,2,1,0:T(8,128)(2,1)S(1)}, bf16[4,2,512,128]{3,2,1,0:T(8,128)(2,1)}, u32[]{:S(2)}, u32[]{:S(2)}) collective-permute-start(bf16[4,2,512,128]{3,2,1,0:T(8,128)(2,1)S(1)} %copy-done.5), channel_id=1, source_target_pairs={{0,12},{1,13},{2,14},{3,15},{4,8},{5,9},{6,10},{7,11},{8,4},{9,5},... | collective-permute-start | bytes 3145736 | tf_op jit(solution)/shard_map/ppermute | solution.py:258
  231.2 109.0 %collective-permute-start.8 = (bf16[4,2,512,128]{3,2,1,0:T(8,128)(2,1)S(1)}, bf16[4,2,512,128]{3,2,1,0:T(8,128)(2,1)}, u32[]{:S(2)}, u32[]{:S(2)}) collective-permute-start(bf16[4,2,512,128]{3,2,1,0:T(8,128)(2,1)S(1)} %copy-done.4), channel_id=1, source_target_pairs={{0,13},{1,12},{2,15},{3,14},{4,9},{5,8},{6,11},{7,10},{8,5},{9,4},... | collective-permute-start | bytes 3145736 | tf_op jit(solution)/shard_map/ppermute | solution.py:258
  236.9 124.2 %collective-permute-start.7 = (bf16[4,2,512,128]{3,2,1,0:T(8,128)(2,1)S(1)}, bf16[4,2,512,128]{3,2,1,0:T(8,128)(2,1)}, u32[]{:S(2)}, u32[]{:S(2)}) collective-permute-start(bf16[4,2,512,128]{3,2,1,0:T(8,128)(2,1)S(1)} %copy-done.3), channel_id=1, source_target_pairs={{0,14},{1,15},{2,12},{3,13},{4,10},{5,11},{6,8},{7,9},{8,6},{9,7},... | collective-permute-start | bytes 3145736 | tf_op jit(solution)/shard_map/ppermute | solution.py:258
  238.9 145.4 %collective-permute-start = (bf16[4,2,512,128]{3,2,1,0:T(8,128)(2,1)}, bf16[4,2,512,128]{3,2,1,0:T(8,128)(2,1)}, u32[]{:S(2)}, u32[]{:S(2)}) collective-permute-start(bf16[4,2,512,128]{3,2,1,0:T(8,128)(2,1)} %gather_units.16), channel_id=1, source_target_pairs={{0,15},{1,14},{2,13},{3,12},{4,11},{5,10},{6,9},{7,8},{8,7},{9,6},... | collective-permute-start | bytes 3145736 | tf_op jit(solution)/shard_map/ppermute | solution.py:258
where the time goes:
time: 392 us; the launch traced here: 389 us
  waiting for transfers between devices  229 us (58%)
  Pallas kernels  122 us (31%)
  starting transfers between devices  30.6 us (8%)
  local copies, waits for them, and re-layouts  6.4 us (2%)
    ppermute x15, waiting for transfers between devices, local(): arrived[offset] = lax.ppermute(units, 'wide', pairs_of(offset))  146 us
    ppermute x6, waiting for transfers between devices, go_round(): lax.ppermute(tokens, 'wide', pairs_of(step * stride))  82.7 us
    pallas_call x16, Pallas kernels, absorb(): pl.pallas_call(functools.partial(absorb_body, offset, per_device, head_co...  78.5 us
    pallas_call x16, Pallas kernels, gather_units(): pl.pallas_call(functools.partial(gather_body, offset, per_device, head_co...  43.2 us
    ppermute x15, starting transfers between devices, local(): arrived[offset] = lax.ppermute(units, 'wide', pairs_of(offset))  24.7 us
  transfers between devices with their start and end apart: 21, of which 10 were waited for; matrix products, arithmetic and copies ran while one was open for 2% of the time, Pallas kernels for 29%

commit v1 on v0

--- a/solution.py
+++ b/solution.py
@@ -27,8 +27,10 @@
 
 
 def gather_body(
-    offset, per_device, head_count, dense, me_ref, slots_ref, lengths_ref, kv_ref, sent_ref, held_ref, in_sem, out_sem
+    offset, per_device, head_count, dense, me_ref, slots_ref, lengths_ref, kv_ref, *refs
 ):
+    *outs, held_ref, in_sem, out_sem = refs
+    places = [ref.at[unit] for ref in outs for unit in range(ref.shape[0])]
     rows = kv_ref.shape[2]
     me = me_ref[0]
     items, limits = slot_lengths(slots_ref, lengths_ref, me ^ offset, per_device, head_count)
@@ -45,22 +47,22 @@
         pltpu.make_async_copy(kv_ref.at[:, item], held_ref.at[unit], in_sem.at[unit]).start()
     for unit in range(per_device):
         pltpu.make_async_copy(kv_ref.at[:, 0], held_ref.at[unit], in_sem.at[unit]).wait()
-        pltpu.make_async_copy(held_ref.at[unit], sent_ref.at[unit], out_sem.at[unit]).start()
+        pltpu.make_async_copy(held_ref.at[unit], places[unit], out_sem.at[unit]).start()
     for unit in range(per_device):
-        pltpu.make_async_copy(held_ref.at[unit], sent_ref.at[unit], out_sem.at[unit]).wait()
-
-
-def gather_units(scalars, kv, offset, per_device, head_count, dense):
+        pltpu.make_async_copy(held_ref.at[unit], places[unit], out_sem.at[unit]).wait()
+
+
+def gather_units(scalars, kv, offset, parts, head_count, dense):
     _, _, rows, head_dim = kv.shape
-    unit = (2, rows, head_dim)
+    unit, per_device = (2, rows, head_dim), sum(parts)
     return pl.pallas_call(
         functools.partial(gather_body, offset, per_device, head_count, dense),
-        out_shape=jax.ShapeDtypeStruct((per_device, *unit), kv.dtype),
+        out_shape=[jax.ShapeDtypeStruct((part, *unit), kv.dtype) for part in parts],
         grid_spec=pltpu.PrefetchScalarGridSpec(
             num_scalar_prefetch=3,
             grid=(1,),
             in_specs=[pl.BlockSpec(memory_space=pl.ANY)],
-            out_specs=pl.BlockSpec(memory_space=pl.ANY),
+            out_specs=[pl.BlockSpec(memory_space=pl.ANY)] * len(parts),
             scratch_shapes=[
                 pltpu.VMEM((per_device, *unit), kv.dtype),
                 pltpu.SemaphoreType.DMA((per_device,)),
@@ -76,8 +78,12 @@
     )(*scalars, kv)
 
 
+def heads_side_by_side(mean):
+    return jnp.concatenate([mean[head : head + 1] for head in range(mean.shape[0])], axis=1)
+
+
 def absorb_body(
-    offset, per_device, head_count, scale, dense, first, last, me_ref, slots_ref, lengths_ref, recv_ref, *refs
+    offset, per_device, head_count, scale, dense, first, last, active, me_ref, slots_ref, lengths_ref, recv_ref, *refs
 ):
     if first:
         token_ref, cache_ref, state_ref, held_ref, in_sem, out_sem = refs
@@ -89,36 +95,36 @@
     start = (me ^ offset) * rows
     _, limits = slot_lengths(slots_ref, lengths_ref, me, per_device, head_count)
     held, ranks = rank_of(limits, start)
-    for slot in range(per_device):
-        unit = slot if dense else ranks[slot]
+    for slot in active:
+        unit = slot - active[0] if dense else ranks[slot]
 
         @pl.when(held[slot] == 1)
         def _():
-            pltpu.make_async_copy(recv_ref.at[unit], held_ref.at[slot], in_sem.at[slot]).start()
-
-    for slot in range(per_device):
+            pltpu.make_async_copy(recv_ref.at[unit], held_ref.at[slot - active[0]], in_sem.at[slot]).start()
+
+    for slot in active:
         limit = limits[slot] - start
 
         @pl.when(limit > 0)
         def _():
-            pltpu.make_async_copy(recv_ref.at[0], held_ref.at[slot], in_sem.at[slot]).wait()
+            pltpu.make_async_copy(recv_ref.at[0], held_ref.at[slot - active[0]], in_sem.at[slot]).wait()
 
         @pl.when(limit <= 0)
         def _():
-            held_ref[slot] = jnp.zeros_like(held_ref[slot])
+            held_ref[slot - active[0]] = jnp.zeros_like(held_ref[slot - active[0]])
 
         @pl.when((limit >= 0) & (limit < rows))
         def _():
             row = lax.broadcasted_iota(jnp.int32, (rows, head_dim), 0)
             for part in range(2):
                 fresh = token_ref[slot, group + part : group + part + 1, :].astype(jnp.float32)
-                block = held_ref[slot, part].astype(jnp.float32)
+                block = held_ref[slot - active[0], part].astype(jnp.float32)
                 block = jnp.where(row < limit, block, jnp.where(row == limit, fresh, 0.0))
-                held_ref[slot, part] = block.astype(held_ref.dtype)
+                held_ref[slot - active[0], part] = block.astype(held_ref.dtype)
 
         for part in range(2):
             pltpu.make_async_copy(
-                held_ref.at[slot, part],
+                held_ref.at[slot - active[0], part],
                 cache_ref.at[part, slot, pl.ds(pl.multiple_of(start, rows), rows)],
                 out_sem.at[slot, part],
             ).start()
@@ -132,9 +138,17 @@
             old_out = jnp.zeros((group, head_dim), jnp.float32)
         else:
             old_max, old_sum, old_out = old_ref[0, slot], old_ref[1, slot], old_ref[2, slot]
+        if slot not in active:
+            if last:
+                outputs.append(heads_side_by_side(old_out / old_sum))
+            else:
+                state_ref[0, slot] = old_max
+                state_ref[1, slot] = old_sum
+                state_ref[2, slot] = old_out
+            continue
         query = token_ref[slot, :group, :]
         scores = lax.dot_general(
-            query, held_ref[slot, 0], (((1,), (1,)), ((), ())), preferred_element_type=jnp.float32
+            query, held_ref[slot - active[0], 0], (((1,), (1,)), ((), ())), preferred_element_type=jnp.float32
         )
         scores = scores * scale
         visible = lax.broadcasted_iota(jnp.int32, scores.shape, 1) <= limit
@@ -146,16 +160,14 @@
         rest = weights - high.astype(jnp.float32)
         middle = rest.astype(jnp.bfloat16)
         low = (rest - middle.astype(jnp.float32)).astype(jnp.bfloat16)
-        value = held_ref[slot, 1]
+        value = held_ref[slot - active[0], 1]
         summed = sum(
             jnp.dot(term, value, preferred_element_type=jnp.float32) for term in (low, middle, high)
         )
         new_sum = old_sum * factor + jnp.sum(weights, axis=1, keepdims=True)
         new_out = old_out * factor + summed
         if last:
-            mean = new_out / new_sum
-            heads = [mean[head : head + 1] for head in range(group)]
-            outputs.append(jnp.concatenate(heads, axis=1))
+            outputs.append(heads_side_by_side(new_out / new_sum))
         else:
             state_ref[0, slot] = new_max
             state_ref[1, slot] = new_sum
@@ -163,24 +175,25 @@
     if last:
         state_ref[...] = jnp.concatenate(outputs, axis=0).astype(state_ref.dtype)
 
-    for slot in range(per_device):
+    for slot in active:
         for part in range(2):
             pltpu.make_async_copy(
-                held_ref.at[slot, part],
+                held_ref.at[slot - active[0], part],
                 cache_ref.at[part, slot, pl.ds(pl.multiple_of(start, rows), rows)],
                 out_sem.at[slot, part],
             ).wait()
 
 
-def absorb(scalars, recv, tokens, carry, offset, head_count, devices, dense, last):
-    per_device, _, rows, head_dim = recv.shape
+def absorb(scalars, recv, tokens, carry, offset, head_count, devices, dense, last, active):
+    _, _, rows, head_dim = recv.shape
+    per_device = tokens.shape[0]
     group = tokens.shape[1] - 2
     first = carry is None
     anywhere, whole = pl.BlockSpec(memory_space=pl.ANY), pl.BlockSpec(memory_space=pltpu.VMEM)
     dtype = recv.dtype
     return pl.pallas_call(
         functools.partial(
-            absorb_body, offset, per_device, head_count, 1.0 / math.sqrt(head_dim), dense, first, last
+            absorb_body, offset, per_device, head_count, 1.0 / math.sqrt(head_dim), dense, first, last, active
         ),
         out_shape=[
             jax.ShapeDtypeStruct((2, per_device, rows * devices, head_dim), dtype),
@@ -194,7 +207,7 @@
             in_specs=[anywhere, whole] + ([] if first else [anywhere, whole]),
             out_specs=[anywhere, whole],
             scratch_shapes=[
-                pltpu.VMEM((per_device, 2, rows, head_dim), dtype),
+                pltpu.VMEM((len(active), 2, rows, head_dim), dtype),
                 pltpu.SemaphoreType.DMA((per_device,)),
                 pltpu.SemaphoreType.DMA((per_device, 2)),
             ],
@@ -239,10 +252,16 @@
         *near[quarter:],
         *far[quarter:],
     ]
+
+    def parts_of(offset):
+        first = (per_device + 1) // 2
+        split = offset == order[-1] and per_device > 1
+        return [first, per_device - first] if split else [per_device]
+
     early = 1
     for offset in order[:early]:
-        units = gather_units(scalars, kv, offset, per_device, head_count, True)
-        arrived[offset] = lax.ppermute(units, "wide", pairs_of(offset))
+        units = gather_units(scalars, kv, offset, parts_of(offset), head_count, True)
+        arrived[offset] = [lax.ppermute(part, "wide", pairs_of(offset)) for part in units]
     units, queries, fresh_kv = lax.optimization_barrier((units, queries, fresh_kv))
     tokens = jnp.concatenate(
         [queries.reshape(per_device, group_size, head_dim), jnp.swapaxes(fresh_kv, 0, 1)], axis=1
@@ -254,26 +273,32 @@
         tokens = go_round(tokens, stride, steps)
         stride *= steps
     for offset in order[early:]:
-        units = gather_units(scalars, kv, offset, per_device, head_count, True)
-        arrived[offset] = lax.ppermute(units, "wide", pairs_of(offset))
-    arrived[0] = gather_units(scalars, kv, 0, per_device, head_count, True)
+        units = gather_units(scalars, kv, offset, parts_of(offset), head_count, True)
+        arrived[offset] = [lax.ppermute(part, "wide", pairs_of(offset)) for part in units]
+    arrived[0] = gather_units(scalars, kv, 0, [per_device], head_count, True)
     own_slots = lax.dynamic_slice_in_dim(decode_slot_pair, rank * per_device, per_device)
     rows = ((own_slots // per_device) ^ rank) * per_device + own_slots % per_device
     own_tokens = jnp.take(tokens, rows, axis=0)
 
     carry = None
     for offset in [0, *order]:
-        carry = absorb(
-            scalars,
-            arrived[offset],
-            own_tokens,
-            carry,
-            offset,
-            head_count,
-            devices,
-            dense[offset],
-            offset == order[-1],
-        )
+        done = 0
+        for part in arrived[offset]:
+            active = range(done, done + part.shape[0])
+            done = active.stop
+            last = offset == order[-1] and done == per_device
+            carry = absorb(
+                scalars,
+                part,
+                own_tokens,
+                carry,
+                offset,
+                head_count,
+                devices,
+                dense[offset],
+                last,
+                active,
+            )
     return tuple(carry)
 
 

time: 392 us -> 391 us (level)
  waiting for transfers between devices: 229 us -> 218 us
  starting transfers between devices: 30.6 us -> 37.2 us
    ppermute x15 -> x16, waiting for transfers between devices: 146 us -> 140 us  [local(): lax.ppermute(part, 'wide', pairs_of(offset))]
    ppermute x15 -> x16, starting transfers between devices: 24.7 us -> 29.6 us  [local(): lax.ppermute(part, 'wide', pairs_of(offset))]
    ppermute x6, waiting for transfers between devices: 82.7 us -> 78.1 us  [go_round(): lax.ppermute(tokens, 'wide', pairs_of(step * stride))]
    pallas_call x16 -> x17, Pallas kernels: 78.5 us -> 81.7 us  [absorb(): pl.pallas_call(functools.partial(absorb_body, offset, per_device, head_co...]
  transfers between devices with their start and end apart: 21 -> 22, of which waited for: 10 -> 16; matrix products, arithmetic and copies ran while one was open for 2% -> 2% of each run, Pallas kernels for 29% -> 30%
where the time goes in v1:
time: 391 us; the launch traced here: 388 us
  waiting for transfers between devices  218 us (56%)
  Pallas kernels  125 us (32%)
  starting transfers between devices  37.2 us (10%)
  local copies, waits for them, and re-layouts  6.46 us (2%)
    ppermute x16, waiting for transfers between devices, local(): lax.ppermute(part, 'wide', pairs_of(offset))  140 us
    pallas_call x17, Pallas kernels, absorb(): pl.pallas_call(functools.partial(absorb_body, offset, per_device, head_co...  81.7 us
    ppermute x6, waiting for transfers between devices, go_round(): lax.ppermute(tokens, 'wide', pairs_of(step * stride))  78.1 us
    pallas_call x16, Pallas kernels, gather_units(): pl.pallas_call(functools.partial(gather_body, offset, per_device, head_co...  43.2 us
    ppermute x16, starting transfers between devices, local(): lax.ppermute(part, 'wide', pairs_of(offset))  29.6 us
  transfers between devices with their start and end apart: 22, of which 16 were waited for; matrix products, arithmetic and copies ran while one was open for 2% of the time, Pallas kernels for 30%

profile of v1, /device:TPU:9, one launch (start us, length us, event | category | flops | bytes accessed | tf_op | source)
XLA Modules:
  0.0 388.2 jit_solution(11421889288809742314)
XLA Ops:
  0.6 2.7 gather_units.17
  3.3 2.4 collective-permute-start.21
  5.7 2.7 gather_units.30
  8.6 2.7 gather_units.29
  11.3 0.9 collective-permute-start.19
  12.3 2.7 gather_units.28
  15.0 1.6 collective-permute-start.18
  18.3 0.8 collective-permute-done.1
  19.1 1.2 collective-permute-start.2
  20.3 1.7 collective-permute-done.2
  22.1 2.2 collective-permute-start.3
  24.3 1.9 collective-permute-done.3
  26.4 71.7 %collective-permute-done.4 = bf16[16,10,128]{2,1,0:T(8,128)(2,1)S(1)} collective-permute-done((bf16[16,10,128]{2,1,0:T(8,128)(2,1)S(1)}, bf16[16,10,128]{2,1,0:T(8,128)(2,1)S(1)}, u32[]{:S(2)}, u32[]{:S(2)}) %collective-permute-start.4) | collective-permute-done | bytes 40992 | tf_op jit(solution)/shard_map/ppermute | solution.py:240
  98.1 2.9 collective-permute-start.5
  100.9 1.7 collective-permute-done.5
  103.3 2.7 gather_units.27
  106.3 4.5 %collective-permute-start.17 = (bf16[4,2,512,128]{3,2,1,0:T(8,128)(2,1)}, bf16[4,2,512,128]{3,2,1,0:T(8,128)(2,1)}, u32[]{:S(2)}, u32[]{:S(2)}) collective-permute-start(bf16[4,2,512,128]{3,2,1,0:T(8,128)(2,1)} %gather_units.27), channel_id=1, source_target_pairs={{0,10},{1,11},{2,8},{3,9},{4,14},{5,15},{6,12},{7,13},{8,2},{9,3},... | collective-permute-start | bytes 3145736 | tf_op jit(solution)/shard_map/ppermute | solution.py:277
  110.8 2.7 gather_units.26
  113.6 2.7 gather_units.25
  116.2 2.7 gather_units.24
  118.9 2.7 gather_units.23
  121.7 8.7 %collective-permute-start.15 = (bf16[4,2,512,128]{3,2,1,0:T(8,128)(2,1)}, bf16[4,2,512,128]{3,2,1,0:T(8,128)(2,1)}, u32[]{:S(2)}, u32[]{:S(2)}) collective-permute-start(bf16[4,2,512,128]{3,2,1,0:T(8,128)(2,1)} %gather_units.25), channel_id=1, source_target_pairs={{0,11},{1,10},{2,9},{3,8},{4,15},{5,14},{6,13},{7,12},{8,3},{9,2},... | collective-permute-start | bytes 3145736 | tf_op jit(solution)/shard_map/ppermute | solution.py:277
  130.5 2.7 gather_units.22
  133.3 26.0 %collective-permute-done.17.recv_ref = bf16[4,2,512,128]{3,2,1,0:T(8,128)(2,1)} collective-permute-done((bf16[4,2,512,128]{3,2,1,0:T(8,128)(2,1)}, bf16[4,2,512,128]{3,2,1,0:T(8,128)(2,1)}, u32[]{:S(2)}, u32[]{:S(2)}) %collective-permute-start.17) | collective-permute-done | bytes 1048608 | tf_op jit(solution)/shard_map/ppermute | solution.py:277
  159.2 1.3 collective-permute-start.12
  160.6 2.7 gather_units.21
  163.3 3.1 collective-permute-start.11
  166.4 2.7 gather_units.31.recv_ref
  169.1 2.7 gather_units.20
  171.8 2.7 gather_units.19
  174.5 2.8 gather_units.18
  177.3 2.8 gather_units.16
  180.8 19.7 %collective-permute-done.15.recv_ref = bf16[4,2,512,128]{3,2,1,0:T(8,128)(2,1)} collective-permute-done((bf16[4,2,512,128]{3,2,1,0:T(8,128)(2,1)}, bf16[4,2,512,128]{3,2,1,0:T(8,128)(2,1)}, u32[]{:S(2)}, u32[]{:S(2)}) %collective-permute-start.15) | collective-permute-done | bytes 1048608 | tf_op jit(solution)/shard_map/ppermute | solution.py:277
  200.5 0.8 collective-permute-start.10
  201.3 2.0 collective-permute-done.14.recv_ref
  203.2 2.0 collective-permute-start.9
  205.2 0.7 collective-permute-start.8
  209.0 1.5 gather_fusion
  210.5 14.7 %collective-permute-done.12.recv_ref = bf16[4,2,512,128]{3,2,1,0:T(8,128)(2,1)} collective-permute-done((bf16[4,2,512,128]{3,2,1,0:T(8,128)(2,1)}, bf16[4,2,512,128]{3,2,1,0:T(8,128)(2,1)}, u32[]{:S(2)}, u32[]{:S(2)}) %collective-permute-start.12) | collective-permute-done | bytes 1048608 | tf_op jit(solution)/shard_map/ppermute | solution.py:277
  225.2 1.9 collective-permute-start.7
  227.1 20.9 %collective-permute-done.11.recv_ref = bf16[4,2,512,128]{3,2,1,0:T(8,128)(2,1)S(1)} collective-permute-done((bf16[4,2,512,128]{3,2,1,0:T(8,128)(2,1)}, bf16[4,2,512,128]{3,2,1,0:T(8,128)(2,1)S(1)}, u32[]{:S(2)}, u32[]{:S(2)}) %collective-permute-start.11) | collective-permute-done | bytes 1048608 | tf_op jit(solution)/shard_map/ppermute | solution.py:277
  248.0 1.2 collective-permute-start
  249.9 4.5 %absorb.17 = (bf16[2,4,8192,128]{3,2,1,0:T(8,128)(2,1)}, f32[3,4,8,128]{3,2,1,0:T(8,128)}) custom-call(s32[1]{0:T(128)} %bitcast.me_ref, s32[64]{0:T(128)} %slots_ref.65, s32[8]{0:T(128)} %lengths_ref.65, bf16[4,2,512,128]{3,2,1,0:T(8,128)(2,1)} %gather_units.31.recv_ref, bf16[4,10,128]{2,1,0:T(8,128)(2,1)} %broadcast_select_fusion.refs_0_), custom_call_target="tpu_custom_call" | custom-call | flops 268435456 | bytes 2097152 | tf_op jit(solution)/shard_map/absorb/pallas_call | solution.py:194
  254.5 5.0 %absorb.18 = (bf16[2,4,8192,128]{3,2,1,0:T(8,128)(2,1)}, f32[3,4,8,128]{3,2,1,0:T(8,128)}) custom-call(s32[1]{0:T(128)} %bitcast.me_ref, s32[64]{0:T(128)} %slots_ref.65, s32[8]{0:T(128)} %lengths_ref.65, bf16[4,2,512,128]{3,2,1,0:T(8,128)(2,1)} %collective-permute-done.21.recv_ref, ...), custom_call_target="tpu_custom_call", output_to_operand_aliasing={{0}: (5, {}), {1}: (6, {})} | custom-call | flops 268435456 | bytes 2097152 | tf_op jit(solution)/shard_map/absorb/pallas_call | solution.py:194
  259.4 4.9 %absorb.19 = (bf16[2,4,8192,128]{3,2,1,0:T(8,128)(2,1)}, f32[3,4,8,128]{3,2,1,0:T(8,128)}) custom-call(s32[1]{0:T(128)} %bitcast.me_ref, s32[64]{0:T(128)} %slots_ref.65, s32[8]{0:T(128)} %lengths_ref.65, bf16[4,2,512,128]{3,2,1,0:T(8,128)(2,1)} %copy-done.2, ...), custom_call_target="tpu_custom_call", output_to_operand_aliasing={{0}: (5, {}), {1}: (6, {})} | custom-call | flops 268435456 | bytes 2097152 | tf_op jit(solution)/shard_map/absorb/pallas_call | solution.py:194
  264.4 4.9 %absorb.20 = (bf16[2,4,8192,128]{3,2,1,0:T(8,128)(2,1)}, f32[3,4,8,128]{3,2,1,0:T(8,128)}) custom-call(s32[1]{0:T(128)} %bitcast.me_ref, s32[64]{0:T(128)} %slots_ref.65, s32[8]{0:T(128)} %lengths_ref.65, bf16[4,2,512,128]{3,2,1,0:T(8,128)(2,1)} %copy-done.1, ...), custom_call_target="tpu_custom_call", output_to_operand_aliasing={{0}: (5, {}), {1}: (6, {})} | custom-call | flops 268435456 | bytes 2097152 | tf_op jit(solution)/shard_map/absorb/pallas_call | solution.py:194
  269.3 4.9 %absorb.21 = (bf16[2,4,8192,128]{3,2,1,0:T(8,128)(2,1)}, f32[3,4,8,128]{3,2,1,0:T(8,128)}) custom-call(s32[1]{0:T(128)} %bitcast.me_ref, s32[64]{0:T(128)} %slots_ref.65, s32[8]{0:T(128)} %lengths_ref.65, bf16[4,2,512,128]{3,2,1,0:T(8,128)(2,1)} %copy-done, ...), custom_call_target="tpu_custom_call", output_to_operand_aliasing={{0}: (5, {}), {1}: (6, {})} | custom-call | flops 268435456 | bytes 2097152 | tf_op jit(solution)/shard_map/absorb/pallas_call | solution.py:194
  274.2 5.1 %absorb.22 = (bf16[2,4,8192,128]{3,2,1,0:T(8,128)(2,1)}, f32[3,4,8,128]{3,2,1,0:T(8,128)}) custom-call(s32[1]{0:T(128)} %bitcast.me_ref, s32[64]{0:T(128)} %slots_ref.65, s32[8]{0:T(128)} %lengths_ref.65, bf16[4,2,512,128]{3,2,1,0:T(8,128)(2,1)} %collective-permute-done.17.recv_ref, ...), custom_call_target="tpu_custom_call", output_to_operand_aliasing={{0}: (5, {}), {1}: (6, {})} | custom-call | flops 268435456 | bytes 2097152 | tf_op jit(solution)/shard_map/absorb/pallas_call | solution.py:194
  279.3 4.9 %absorb.23 = (bf16[2,4,8192,128]{3,2,1,0:T(8,128)(2,1)}, f32[3,4,8,128]{3,2,1,0:T(8,128)}) custom-call(s32[1]{0:T(128)} %bitcast.me_ref, s32[64]{0:T(128)} %slots_ref.65, s32[8]{0:T(128)} %lengths_ref.65, bf16[4,2,512,128]{3,2,1,0:T(8,128)(2,1)} %collective-permute-done.16.recv_ref, ...), custom_call_target="tpu_custom_call", output_to_operand_aliasing={{0}: (5, {}), {1}: (6, {})} | custom-call | flops 268435456 | bytes 2097152 | tf_op jit(solution)/shard_map/absorb/pallas_call | solution.py:194
  284.3 5.0 %absorb.24 = (bf16[2,4,8192,128]{3,2,1,0:T(8,128)(2,1)}, f32[3,4,8,128]{3,2,1,0:T(8,128)}) custom-call(s32[1]{0:T(128)} %bitcast.me_ref, s32[64]{0:T(128)} %slots_ref.65, s32[8]{0:T(128)} %lengths_ref.65, bf16[4,2,512,128]{3,2,1,0:T(8,128)(2,1)} %collective-permute-done.15.recv_ref, ...), custom_call_target="tpu_custom_call", output_to_operand_aliasing={{0}: (5, {}), {1}: (6, {})} | custom-call | flops 268435456 | bytes 2097152 | tf_op jit(solution)/shard_map/absorb/pallas_call | solution.py:194
  289.2 4.9 %absorb.25 = (bf16[2,4,8192,128]{3,2,1,0:T(8,128)(2,1)}, f32[3,4,8,128]{3,2,1,0:T(8,128)}) custom-call(s32[1]{0:T(128)} %bitcast.me_ref, s32[64]{0:T(128)} %slots_ref.65, s32[8]{0:T(128)} %lengths_ref.65, bf16[4,2,512,128]{3,2,1,0:T(8,128)(2,1)} %collective-permute-done.14.recv_ref, ...), custom_call_target="tpu_custom_call", output_to_operand_aliasing={{0}: (5, {}), {1}: (6, {})} | custom-call | flops 268435456 | bytes 2097152 | tf_op jit(solution)/shard_map/absorb/pallas_call | solution.py:194
  294.2 4.9 %absorb.26 = (bf16[2,4,8192,128]{3,2,1,0:T(8,128)(2,1)}, f32[3,4,8,128]{3,2,1,0:T(8,128)}) custom-call(s32[1]{0:T(128)} %bitcast.me_ref, s32[64]{0:T(128)} %slots_ref.65, s32[8]{0:T(128)} %lengths_ref.65, bf16[4,2,512,128]{3,2,1,0:T(8,128)(2,1)} %collective-permute-done.13.recv_ref, ...), custom_call_target="tpu_custom_call", output_to_operand_aliasing={{0}: (5, {}), {1}: (6, {})} | custom-call | flops 268435456 | bytes 2097152 | tf_op jit(solution)/shard_map/absorb/pallas_call | solution.py:194
  299.1 4.9 %absorb.27 = (bf16[2,4,8192,128]{3,2,1,0:T(8,128)(2,1)}, f32[3,4,8,128]{3,2,1,0:T(8,128)}) custom-call(s32[1]{0:T(128)} %bitcast.me_ref, s32[64]{0:T(128)} %slots_ref.65, s32[8]{0:T(128)} %lengths_ref.65, bf16[4,2,512,128]{3,2,1,0:T(8,128)(2,1)} %collective-permute-done.12.recv_ref, ...), custom_call_target="tpu_custom_call", output_to_operand_aliasing={{0}: (5, {}), {1}: (6, {})} | custom-call | flops 268435456 | bytes 2097152 | tf_op jit(solution)/shard_map/absorb/pallas_call | solution.py:194
  304.0 4.9 %absorb.28 = (bf16[2,4,8192,128]{3,2,1,0:T(8,128)(2,1)}, f32[3,4,8,128]{3,2,1,0:T(8,128)}) custom-call(s32[1]{0:T(128)} %bitcast.me_ref, s32[64]{0:T(128)} %slots_ref.65, s32[8]{0:T(128)} %lengths_ref.65, bf16[4,2,512,128]{3,2,1,0:T(8,128)(2,1)} %copy-done.5, ...), custom_call_target="tpu_custom_call", output_to_operand_aliasing={{0}: (5, {}), {1}: (6, {})} | custom-call | flops 268435456 | bytes 2097152 | tf_op jit(solution)/shard_map/absorb/pallas_call | solution.py:194
  308.9 6.0 %collective-permute-done.10.recv_ref = bf16[4,2,512,128]{3,2,1,0:T(8,128)(2,1)} collective-permute-done((bf16[4,2,512,128]{3,2,1,0:T(8,128)(2,1)}, bf16[4,2,512,128]{3,2,1,0:T(8,128)(2,1)}, u32[]{:S(2)}, u32[]{:S(2)}) %collective-permute-start.10) | collective-permute-done | bytes 1048608 | tf_op jit(solution)/shard_map/ppermute | solution.py:277
  314.9 4.9 %absorb.29 = (bf16[2,4,8192,128]{3,2,1,0:T(8,128)(2,1)}, f32[3,4,8,128]{3,2,1,0:T(8,128)}) custom-call(s32[1]{0:T(128)} %bitcast.me_ref, s32[64]{0:T(128)} %slots_ref.65, s32[8]{0:T(128)} %lengths_ref.65, bf16[4,2,512,128]{3,2,1,0:T(8,128)(2,1)} %collective-permute-done.10.recv_ref, ...), custom_call_target="tpu_custom_call", output_to_operand_aliasing={{0}: (5, {}), {1}: (6, {})} | custom-call | flops 268435456 | bytes 2097152 | tf_op jit(solution)/shard_map/absorb/pallas_call | solution.py:194
  319.8 19.2 %collective-permute-done.9.recv_ref = bf16[4,2,512,128]{3,2,1,0:T(8,128)(2,1)} collective-permute-done((bf16[4,2,512,128]{3,2,1,0:T(8,128)(2,1)S(1)}, bf16[4,2,512,128]{3,2,1,0:T(8,128)(2,1)}, u32[]{:S(2)}, u32[]{:S(2)}) %collective-permute-start.9) | collective-permute-done | bytes 1048608 | tf_op jit(solution)/shard_map/ppermute | solution.py:277
  339.0 4.9 %absorb.30 = (bf16[2,4,8192,128]{3,2,1,0:T(8,128)(2,1)}, f32[3,4,8,128]{3,2,1,0:T(8,128)}) custom-call(s32[1]{0:T(128)} %bitcast.me_ref, s32[64]{0:T(128)} %slots_ref.65, s32[8]{0:T(128)} %lengths_ref.65, bf16[4,2,512,128]{3,2,1,0:T(8,128)(2,1)} %collective-permute-done.9.recv_ref, ...), custom_call_target="tpu_custom_call", output_to_operand_aliasing={{0}: (5, {}), {1}: (6, {})} | custom-call | flops 268435456 | bytes 2097152 | tf_op jit(solution)/shard_map/absorb/pallas_call | solution.py:194
  343.9 16.9 %collective-permute-done.8.recv_ref = bf16[4,2,512,128]{3,2,1,0:T(8,128)(2,1)} collective-permute-done((bf16[4,2,512,128]{3,2,1,0:T(8,128)(2,1)S(1)}, bf16[4,2,512,128]{3,2,1,0:T(8,128)(2,1)}, u32[]{:S(2)}, u32[]{:S(2)}) %collective-permute-start.8) | collective-permute-done | bytes 1048608 | tf_op jit(solution)/shard_map/ppermute | solution.py:277
  360.8 4.9 %absorb.31 = (bf16[2,4,8192,128]{3,2,1,0:T(8,128)(2,1)}, f32[3,4,8,128]{3,2,1,0:T(8,128)}) custom-call(s32[1]{0:T(128)} %bitcast.me_ref, s32[64]{0:T(128)} %slots_ref.65, s32[8]{0:T(128)} %lengths_ref.65, bf16[4,2,512,128]{3,2,1,0:T(8,128)(2,1)} %collective-permute-done.8.recv_ref, ...), custom_call_target="tpu_custom_call", output_to_operand_aliasing={{0}: (5, {}), {1}: (6, {})} | custom-call | flops 268435456 | bytes 2097152 | tf_op jit(solution)/shard_map/absorb/pallas_call | solution.py:194
  365.7 8.2 %collective-permute-done.7.recv_ref = bf16[2,2,512,128]{3,2,1,0:T(8,128)(2,1)} collective-permute-done((bf16[2,2,512,128]{3,2,1,0:T(8,128)(2,1)}, bf16[2,2,512,128]{3,2,1,0:T(8,128)(2,1)}, u32[]{:S(2)}, u32[]{:S(2)}) %collective-permute-start.7) | collective-permute-done | bytes 524320 | tf_op jit(solution)/shard_map/ppermute | solution.py:277
  374.0 4.0 %absorb.32 = (bf16[2,4,8192,128]{3,2,1,0:T(8,128)(2,1)}, f32[3,4,8,128]{3,2,1,0:T(8,128)}) custom-call(s32[1]{0:T(128)} %bitcast.me_ref, s32[64]{0:T(128)} %slots_ref.65, s32[8]{0:T(128)} %lengths_ref.65, bf16[2,2,512,128]{3,2,1,0:T(8,128)(2,1)} %collective-permute-done.7.recv_ref, ...), custom_call_target="tpu_custom_call", output_to_operand_aliasing={{0}: (5, {}), {1}: (6, {})} | custom-call | flops 268435456 | bytes 2097152 | tf_op jit(solution)/shard_map/absorb/pallas_call | solution.py:194
  378.0 5.9 %collective-permute-done.recv_ref = bf16[2,2,512,128]{3,2,1,0:T(8,128)(2,1)} collective-permute-done((bf16[2,2,512,128]{3,2,1,0:T(8,128)(2,1)}, bf16[2,2,512,128]{3,2,1,0:T(8,128)(2,1)}, u32[]{:S(2)}, u32[]{:S(2)}) %collective-permute-start) | collective-permute-done | bytes 524320 | tf_op jit(solution)/shard_map/ppermute | solution.py:277
  384.0 4.0 %absorb.33 = (bf16[2,4,8192,128]{3,2,1,0:T(8,128)(2,1)}, bf16[4,1024]{1,0:T(4,128)(2,1)}) custom-call(s32[1]{0:T(128)} %bitcast.me_ref, s32[64]{0:T(128)} %slots_ref.65, s32[8]{0:T(128)} %lengths_ref.65, bf16[2,2,512,128]{3,2,1,0:T(8,128)(2,1)} %collective-permute-done.recv_ref, ...), custom_call_target="tpu_custom_call", output_to_operand_aliasing={{0}: (5, {})} | custom-call | flops 268435456 | bytes 2097152 | tf_op jit(solution)/shard_map/absorb/pallas_call | solution.py:194
  (44 shorter events, 7.7 us)
Async XLA Ops:
  3.3 110.1 %collective-permute-start.21 = (bf16[4,2,512,128]{3,2,1,0:T(8,128)(2,1)}, bf16[4,2,512,128]{3,2,1,0:T(8,128)(2,1)}, u32[]{:S(2)}, u32[]{:S(2)}) collective-permute-start(bf16[4,2,512,128]{3,2,1,0:T(8,128)(2,1)} %gather_units.17), channel_id=1, source_target_pairs={{0,8},{1,9},{2,10},{3,11},{4,12},{5,13},{6,14},{7,15},{8,0},{9,1},... | collective-permute-start | bytes 3145736 | tf_op jit(solution)/shard_map/ppermute | solution.py:264
  8.4 8.3 %copy-start.7 = (bf16[4,1024]{1,0:T(4,128)(2,1)S(1)}, bf16[4,1024]{1,0:T(4,128)(2,1)}, u32[]{:S(2)}) copy-start(bf16[4,1024]{1,0:T(4,128)(2,1)} %param.6) | copy-start | bytes 24580
  8.4 8.8 %copy-start.8 = (bf16[2,4,128]{2,1,0:T(4,128)(2,1)S(1)}, bf16[2,4,128]{2,1,0:T(4,128)(2,1)}, u32[]{:S(2)}) copy-start(bf16[2,4,128]{2,1,0:T(4,128)(2,1)} %param.7) | copy-start | bytes 6148
  8.4 113.2 %collective-permute-start.20 = (bf16[4,2,512,128]{3,2,1,0:T(8,128)(2,1)}, bf16[4,2,512,128]{3,2,1,0:T(8,128)(2,1)S(1)}, u32[]{:S(2)}, u32[]{:S(2)}) collective-permute-start(bf16[4,2,512,128]{3,2,1,0:T(8,128)(2,1)} %gather_units.30), channel_id=1, source_target_pairs={{0,4},{1,5},{2,6},{3,7},{4,0},{5,1},{6,2},{7,3},{8,12},{9,13},{10,... | collective-permute-start | bytes 3145736 | tf_op jit(solution)/shard_map/ppermute | solution.py:277
  11.3 119.1 %collective-permute-start.19 = (bf16[4,2,512,128]{3,2,1,0:T(8,128)(2,1)}, bf16[4,2,512,128]{3,2,1,0:T(8,128)(2,1)S(1)}, u32[]{:S(2)}, u32[]{:S(2)}) collective-permute-start(bf16[4,2,512,128]{3,2,1,0:T(8,128)(2,1)} %gather_units.29), channel_id=1, source_target_pairs={{0,9},{1,8},{2,11},{3,10},{4,13},{5,12},{6,15},{7,14},{8,1},{9,0},... | collective-permute-start | bytes 3145736 | tf_op jit(solution)/shard_map/ppermute | solution.py:277
  15.0 115.4 %collective-permute-start.18 = (bf16[4,2,512,128]{3,2,1,0:T(8,128)(2,1)}, bf16[4,2,512,128]{3,2,1,0:T(8,128)(2,1)S(1)}, u32[]{:S(2)}, u32[]{:S(2)}) collective-permute-start(bf16[4,2,512,128]{3,2,1,0:T(8,128)(2,1)} %gather_units.28), channel_id=1, source_target_pairs={{0,5},{1,4},{2,7},{3,6},{4,1},{5,0},{6,3},{7,2},{8,13},{9,12},{10,... | collective-permute-start | bytes 3145736 | tf_op jit(solution)/shard_map/ppermute | solution.py:277
  17.8 1.3 collective-permute-start.1
  19.1 3.0 collective-permute-start.2
  22.1 4.1 %collective-permute-start.3 = (bf16[4,10,128]{2,1,0:T(8,128)(2,1)S(1)}, bf16[4,10,128]{2,1,0:T(8,128)(2,1)S(1)}, u32[]{:S(2)}, u32[]{:S(2)}) collective-permute-start(bf16[4,10,128]{2,1,0:T(8,128)(2,1)S(1)} %get-tuple-element.78), channel_id=1, source_target_pairs={{0,3},{1,2},{2,1},{3,0},{4,7},{5,6},{6,5},{7,4},{8,11},{9,10},{10,... | collective-permute-start | bytes 30728 | tf_op jit(solution)/shard_map/ppermute | solution.py:240
  26.3 71.8 %collective-permute-start.4 = (bf16[16,10,128]{2,1,0:T(8,128)(2,1)S(1)}, bf16[16,10,128]{2,1,0:T(8,128)(2,1)S(1)}, u32[]{:S(2)}, u32[]{:S(2)}) collective-permute-start(bf16[16,10,128]{2,1,0:T(8,128)(2,1)S(1)} %pad_maximum_fusion), channel_id=1, source_target_pairs={{0,4},{1,5},{2,6},{3,7},{4,0},{5,1},{6,2},{7,3},{8,12},{9,13},{10,... | collective-permute-start | bytes 122888 | tf_op jit(solution)/shard_map/ppermute | solution.py:240
  98.1 4.6 %collective-permute-start.5 = (bf16[16,10,128]{2,1,0:T(8,128)(2,1)S(1)}, bf16[16,10,128]{2,1,0:T(8,128)(2,1)S(1)}, u32[]{:S(2)}, u32[]{:S(2)}) collective-permute-start(bf16[16,10,128]{2,1,0:T(8,128)(2,1)S(1)} %pad_maximum_fusion), channel_id=1, source_target_pairs={{0,8},{1,9},{2,10},{3,11},{4,12},{5,13},{6,14},{7,15},{8,0},{9,1},... | collective-permute-start | bytes 122888 | tf_op jit(solution)/shard_map/ppermute | solution.py:240
  102.6 3.6 collective-permute-start.6
  106.3 53.0 %collective-permute-start.17 = (bf16[4,2,512,128]{3,2,1,0:T(8,128)(2,1)}, bf16[4,2,512,128]{3,2,1,0:T(8,128)(2,1)}, u32[]{:S(2)}, u32[]{:S(2)}) collective-permute-start(bf16[4,2,512,128]{3,2,1,0:T(8,128)(2,1)} %gather_units.27), channel_id=1, source_target_pairs={{0,10},{1,11},{2,8},{3,9},{4,14},{5,15},{6,12},{7,13},{8,2},{9,3},... | collective-permute-start | bytes 3145736 | tf_op jit(solution)/shard_map/ppermute | solution.py:277
  113.5 49.8 %collective-permute-start.16 = (bf16[4,2,512,128]{3,2,1,0:T(8,128)(2,1)}, bf16[4,2,512,128]{3,2,1,0:T(8,128)(2,1)}, u32[]{:S(2)}, u32[]{:S(2)}) collective-permute-start(bf16[4,2,512,128]{3,2,1,0:T(8,128)(2,1)} %gather_units.26), channel_id=1, source_target_pairs={{0,6},{1,7},{2,4},{3,5},{4,2},{5,3},{6,0},{7,1},{8,14},{9,15},{10,... | collective-permute-start | bytes 3145736 | tf_op jit(solution)/shard_map/ppermute | solution.py:277
  121.7 41.6 %copy-start.2 = (bf16[4,2,512,128]{3,2,1,0:T(8,128)(2,1)}, bf16[4,2,512,128]{3,2,1,0:T(8,128)(2,1)S(1)}, u32[]{:S(2)}) copy-start(bf16[4,2,512,128]{3,2,1,0:T(8,128)(2,1)S(1)} %collective-permute-done.20.recv_ref) | copy-start | bytes 3145732
  121.7 78.8 %collective-permute-start.15 = (bf16[4,2,512,128]{3,2,1,0:T(8,128)(2,1)}, bf16[4,2,512,128]{3,2,1,0:T(8,128)(2,1)}, u32[]{:S(2)}, u32[]{:S(2)}) collective-permute-start(bf16[4,2,512,128]{3,2,1,0:T(8,128)(2,1)} %gather_units.25), channel_id=1, source_target_pairs={{0,11},{1,10},{2,9},{3,8},{4,15},{5,14},{6,13},{7,12},{8,3},{9,2},... | collective-permute-start | bytes 3145736 | tf_op jit(solution)/shard_map/ppermute | solution.py:277
  130.4 32.9 %copy-start.1 = (bf16[4,2,512,128]{3,2,1,0:T(8,128)(2,1)}, bf16[4,2,512,128]{3,2,1,0:T(8,128)(2,1)S(1)}, u32[]{:S(2)}) copy-start(bf16[4,2,512,128]{3,2,1,0:T(8,128)(2,1)S(1)} %collective-permute-done.19.recv_ref) | copy-start | bytes 3145732
  130.4 72.8 %collective-permute-start.14 = (bf16[4,2,512,128]{3,2,1,0:T(8,128)(2,1)}, bf16[4,2,512,128]{3,2,1,0:T(8,128)(2,1)}, u32[]{:S(2)}, u32[]{:S(2)}) collective-permute-start(bf16[4,2,512,128]{3,2,1,0:T(8,128)(2,1)} %gather_units.24), channel_id=1, source_target_pairs={{0,7},{1,6},{2,5},{3,4},{4,3},{5,2},{6,1},{7,0},{8,15},{9,14},{10,... | collective-permute-start | bytes 3145736 | tf_op jit(solution)/shard_map/ppermute | solution.py:277
  130.4 32.9 %copy-start = (bf16[4,2,512,128]{3,2,1,0:T(8,128)(2,1)}, bf16[4,2,512,128]{3,2,1,0:T(8,128)(2,1)S(1)}, u32[]{:S(2)}) copy-start(bf16[4,2,512,128]{3,2,1,0:T(8,128)(2,1)S(1)} %collective-permute-done.18.recv_ref) | copy-start | bytes 3145732
  130.4 74.8 %collective-permute-start.13 = (bf16[4,2,512,128]{3,2,1,0:T(8,128)(2,1)}, bf16[4,2,512,128]{3,2,1,0:T(8,128)(2,1)}, u32[]{:S(2)}, u32[]{:S(2)}) collective-permute-start(bf16[4,2,512,128]{3,2,1,0:T(8,128)(2,1)} %gather_units.23), channel_id=1, source_target_pairs={{0,1},{1,0},{2,3},{3,2},{4,5},{5,4},{6,7},{7,6},{8,9},{9,8},{10,11... | collective-permute-start | bytes 3145736 | tf_op jit(solution)/shard_map/ppermute | solution.py:277
  159.2 66.0 %collective-permute-start.12 = (bf16[4,2,512,128]{3,2,1,0:T(8,128)(2,1)}, bf16[4,2,512,128]{3,2,1,0:T(8,128)(2,1)}, u32[]{:S(2)}, u32[]{:S(2)}) collective-permute-start(bf16[4,2,512,128]{3,2,1,0:T(8,128)(2,1)} %gather_units.22), channel_id=1, source_target_pairs={{0,2},{1,3},{2,0},{3,1},{4,6},{5,7},{6,4},{7,5},{8,10},{9,11},{10,... | collective-permute-start | bytes 3145736 | tf_op jit(solution)/shard_map/ppermute | solution.py:277
  163.3 84.7 %collective-permute-start.11 = (bf16[4,2,512,128]{3,2,1,0:T(8,128)(2,1)}, bf16[4,2,512,128]{3,2,1,0:T(8,128)(2,1)S(1)}, u32[]{:S(2)}, u32[]{:S(2)}) collective-permute-start(bf16[4,2,512,128]{3,2,1,0:T(8,128)(2,1)} %gather_units.21), channel_id=1, source_target_pairs={{0,3},{1,2},{2,1},{3,0},{4,7},{5,6},{6,5},{7,4},{8,11},{9,10},{10,... | collective-permute-start | bytes 3145736 | tf_op jit(solution)/shard_map/ppermute | solution.py:277
  174.5 5.6 %copy-start.6 = (s32[64]{0:T(128)S(1)}, s32[64]{0:T(128)}, u32[]{:S(2)}) copy-start(s32[64]{0:T(128)} %slots_ref.65) | copy-start | bytes 772
  174.5 28.8 %copy-start.4 = (bf16[4,2,512,128]{3,2,1,0:T(8,128)(2,1)S(1)}, bf16[4,2,512,128]{3,2,1,0:T(8,128)(2,1)}, u32[]{:S(2)}) copy-start(bf16[4,2,512,128]{3,2,1,0:T(8,128)(2,1)} %gather_units.19) | copy-start | bytes 3145732
  177.3 27.9 %copy-start.3 = (bf16[4,2,512,128]{3,2,1,0:T(8,128)(2,1)S(1)}, bf16[4,2,512,128]{3,2,1,0:T(8,128)(2,1)}, u32[]{:S(2)}) copy-start(bf16[4,2,512,128]{3,2,1,0:T(8,128)(2,1)} %gather_units.18) | copy-start | bytes 3145732
  200.5 114.4 %collective-permute-start.10 = (bf16[4,2,512,128]{3,2,1,0:T(8,128)(2,1)}, bf16[4,2,512,128]{3,2,1,0:T(8,128)(2,1)}, u32[]{:S(2)}, u32[]{:S(2)}) collective-permute-start(bf16[4,2,512,128]{3,2,1,0:T(8,128)(2,1)} %gather_units.20), channel_id=1, source_target_pairs={{0,12},{1,13},{2,14},{3,15},{4,8},{5,9},{6,10},{7,11},{8,4},{9,5},... | collective-permute-start | bytes 3145736 | tf_op jit(solution)/shard_map/ppermute | solution.py:277
  203.2 135.8 %collective-permute-start.9 = (bf16[4,2,512,128]{3,2,1,0:T(8,128)(2,1)S(1)}, bf16[4,2,512,128]{3,2,1,0:T(8,128)(2,1)}, u32[]{:S(2)}, u32[]{:S(2)}) collective-permute-start(bf16[4,2,512,128]{3,2,1,0:T(8,128)(2,1)S(1)} %copy-done.4), channel_id=1, source_target_pairs={{0,13},{1,12},{2,15},{3,14},{4,9},{5,8},{6,11},{7,10},{8,5},{9,4},... | collective-permute-start | bytes 3145736 | tf_op jit(solution)/shard_map/ppermute | solution.py:277
  205.2 155.6 %collective-permute-start.8 = (bf16[4,2,512,128]{3,2,1,0:T(8,128)(2,1)S(1)}, bf16[4,2,512,128]{3,2,1,0:T(8,128)(2,1)}, u32[]{:S(2)}, u32[]{:S(2)}) collective-permute-start(bf16[4,2,512,128]{3,2,1,0:T(8,128)(2,1)S(1)} %copy-done.3), channel_id=1, source_target_pairs={{0,14},{1,15},{2,12},{3,13},{4,10},{5,11},{6,8},{7,9},{8,6},{9,7},... | collective-permute-start | bytes 3145736 | tf_op jit(solution)/shard_map/ppermute | solution.py:277
  225.2 148.8 %collective-permute-start.7 = (bf16[2,2,512,128]{3,2,1,0:T(8,128)(2,1)}, bf16[2,2,512,128]{3,2,1,0:T(8,128)(2,1)}, u32[]{:S(2)}, u32[]{:S(2)}) collective-permute-start(bf16[2,2,512,128]{3,2,1,0:T(8,128)(2,1)} %get-tuple-element.41), channel_id=1, source_target_pairs={{0,15},{1,14},{2,13},{3,12},{4,11},{5,10},{6,9},{7,8},{8,7},{9,6},... | collective-permute-start | bytes 1572872 | tf_op jit(solution)/shard_map/ppermute | solution.py:277
  248.0 16.3 %copy-start.5 = (bf16[4,2,512,128]{3,2,1,0:T(8,128)(2,1)}, bf16[4,2,512,128]{3,2,1,0:T(8,128)(2,1)S(1)}, u32[]{:S(2)}) copy-start(bf16[4,2,512,128]{3,2,1,0:T(8,128)(2,1)S(1)} %collective-permute-done.11.recv_ref) | copy-start | bytes 3145732
  248.0 135.9 %collective-permute-start = (bf16[2,2,512,128]{3,2,1,0:T(8,128)(2,1)}, bf16[2,2,512,128]{3,2,1,0:T(8,128)(2,1)}, u32[]{:S(2)}, u32[]{:S(2)}) collective-permute-start(bf16[2,2,512,128]{3,2,1,0:T(8,128)(2,1)} %get-tuple-element.38), channel_id=1, source_target_pairs={{0,15},{1,14},{2,13},{3,12},{4,11},{5,10},{6,9},{7,8},{8,7},{9,6},... | collective-permute-start | bytes 1572872 | tf_op jit(solution)/shard_map/ppermute | solution.py:277
